TPU v7x, 32 devices: a whole 2x2x4 slice. The times are simulated.
32 devices in a mesh: section: 2 (over y), dp: 16 (over z, x, core).
Axes of the slice: x: 2, y: 2, z: 4, core: 2. Of those that a mesh axis runs over, the one named last changes fastest.
Arguments:
- layer_inputs: bfloat16 [2, 4096, 4096], P('section', 'dp'), may hold values from -20 to 20
- norm_gain: float32 [2, 4096], P('section'), may hold values from 0.5 to 1.5
- queries: bfloat16 [2, 4096, 2048], P('section', 'dp'), may hold values from -100 to 100
- output_gradient: bfloat16 [2, 4096, 2048], P('section', 'dp'), may hold values from -6 to 6
- w_key: bfloat16 [2, 4096, 512], P('section'), may hold values from -0.09375 to 0.09375
- value_matrix: bfloat16 [2, 4096, 512], P('section'), may hold values from -0.09375 to 0.09375
- top_grad: bfloat16 [4096, 4096], P('dp'), may hold values from -6 to 6
Outputs:
- key_grad: bfloat16 [2, 4096, 512], P('section')
- value_grad: bfloat16 [2, 4096, 512], P('section')
- input_grad: bfloat16 [2, 4096, 4096], P('section', 'dp')
All inputs are finite; a program needn't handle non-finite values.
Results may differ from a plain program's by a relative error of at most 0.0082.
Values may be sent and summed in bfloat16 or wider, within the bound.
A program may use at most 128 MiB of HBM per device.

v0:
```python
import jax
import jax.numpy as jnp
from jax import lax
from jax.sharding import PartitionSpec as P

HEAD_SIZE = 128
KEY_VALUE_HEADS = 4
SEQUENCE_TOKENS = 128


epsilon = 1e-05


def shifted(value, axis, steps):
    count = lax.axis_size(axis)
    initial, last = (max(0, -steps), min(count, count - steps))
    return lax.ppermute(value, axis, [(source, source + steps) for source in range(initial, last)])


def normalize(block_inputs, gain_row):
    wide_inputs = block_inputs.astype(jnp.float32)
    inv_rms = lax.rsqrt(jnp.mean(wide_inputs * wide_inputs, axis=-1, keepdims=True) + epsilon)
    return (wide_inputs, inv_rms, (wide_inputs * inv_rms * gain_row).astype(jnp.bfloat16))


def value_pass(heads_of_query, heads_of_key, head_gradients):
    scale = HEAD_SIZE ** (-0.5)
    scores = (
        jnp.einsum(
            "btjgd,bsjd->bjgts", heads_of_query, heads_of_key, preferred_element_type=jnp.float32
        )
        * scale
    )
    causal = lax.broadcasted_iota(
        jnp.int32, (SEQUENCE_TOKENS, SEQUENCE_TOKENS), 0
    ) >= lax.broadcasted_iota(jnp.int32, (SEQUENCE_TOKENS, SEQUENCE_TOKENS), 1)
    scores = jnp.where(causal, scores, -1e30)
    row_max = jnp.max(scores, axis=-1, keepdims=True)
    weight = jnp.exp(scores - row_max)
    probability = weight / jnp.sum(weight, axis=-1, keepdims=True)
    value_gradient = jnp.einsum(
        "bjgts,btjgd->bsjd",
        probability.astype(jnp.bfloat16),
        head_gradients,
        preferred_element_type=jnp.float32,
    )
    return (probability, value_gradient.astype(jnp.bfloat16))


def key_pass(probability, heads_of_query, heads_of_value, head_gradients):
    scale = HEAD_SIZE ** (-0.5)
    grad_prob = jnp.einsum(
        "btjgd,bsjd->bjgts", head_gradients, heads_of_value, preferred_element_type=jnp.float32
    )
    row_delta = jnp.sum(probability * grad_prob, axis=-1, keepdims=True)
    dscore = (probability * (grad_prob - row_delta) * scale).astype(jnp.bfloat16)
    key_gradient = jnp.einsum(
        "bjgts,btjgd->bsjd", dscore, heads_of_query, preferred_element_type=jnp.float32
    )
    return key_gradient.astype(jnp.bfloat16)


def weight_term(normed, grad_proj):
    return jnp.einsum("td,tk->dk", normed, grad_proj, preferred_element_type=jnp.float32)


def input_term(
    wide_inputs, inv_rms, gain_row, key_gradient, value_gradient, key_weight, value_weight
):
    grad_norm = jnp.einsum(
        "tk,dk->td", key_gradient, key_weight, preferred_element_type=jnp.float32
    )
    grad_norm = grad_norm + jnp.einsum(
        "tk,dk->td", value_gradient, value_weight, preferred_element_type=jnp.float32
    )
    scaled = gain_row * grad_norm
    return inv_rms * scaled - wide_inputs * inv_rms**3 * jnp.mean(
        wide_inputs * scaled, axis=-1, keepdims=True
    )


def layer_grads(
    block_inputs,
    gain_row,
    block_query_rows,
    block_output_gradient,
    key_weight,
    value_weight,
    value_hook,
):
    wide_inputs, inv_rms, normed = normalize(block_inputs, gain_row)
    key_projected = jnp.dot(normed, key_weight, preferred_element_type=jnp.float32).astype(
        jnp.bfloat16
    )
    value_projected = jnp.dot(normed, value_weight, preferred_element_type=jnp.float32).astype(
        jnp.bfloat16
    )
    count_of_rows = block_inputs.shape[0]
    sequence_count = count_of_rows // SEQUENCE_TOKENS
    heads_of_query = block_query_rows.reshape(
        sequence_count, SEQUENCE_TOKENS, KEY_VALUE_HEADS, -1, HEAD_SIZE
    )
    head_gradients = block_output_gradient.reshape(
        sequence_count, SEQUENCE_TOKENS, KEY_VALUE_HEADS, -1, HEAD_SIZE
    )
    heads_of_key = key_projected.reshape(
        sequence_count, SEQUENCE_TOKENS, KEY_VALUE_HEADS, HEAD_SIZE
    )
    heads_of_value = value_projected.reshape(
        sequence_count, SEQUENCE_TOKENS, KEY_VALUE_HEADS, HEAD_SIZE
    )
    probability, value_gradient = value_pass(heads_of_query, heads_of_key, head_gradients)
    value_gradient = value_gradient.reshape(count_of_rows, KEY_VALUE_HEADS * HEAD_SIZE)
    value_partial = value_hook(weight_term(normed, value_gradient))
    key_gradient = key_pass(probability, heads_of_query, heads_of_value, head_gradients).reshape(
        count_of_rows, KEY_VALUE_HEADS * HEAD_SIZE
    )
    key_partial = weight_term(normed, key_gradient)
    layer_dx = input_term(
        wide_inputs, inv_rms, gain_row, key_gradient, value_gradient, key_weight, value_weight
    )
    return (key_partial, value_partial, layer_dx)


def sum_values(partial_value):
    return lax.psum(partial_value, "dp")


def per_device(layer_inputs, norm_gain, queries, output_gradient, w_key, value_matrix, top_grad):
    layer_count = layer_inputs.shape[0]
    count_of_rows = layer_inputs.shape[1]
    replicas = lax.axis_size("dp")
    is_last = lax.axis_index("section") == lax.axis_size("section") - 1
    residual = jnp.zeros((count_of_rows, layer_inputs.shape[2]), jnp.float32)
    key_sums = [None] * layer_count
    value_sums = [None] * layer_count
    for layer_index in reversed(range(layer_count)):
        key_partial, value_partial, layer_dx = layer_grads(
            layer_inputs[layer_index],
            norm_gain[layer_index],
            queries[layer_index],
            output_gradient[layer_index],
            w_key[layer_index],
            value_matrix[layer_index],
            sum_values,
        )
        key_sums[layer_index] = lax.psum(key_partial, "dp")
        value_sums[layer_index] = value_partial
        residual = layer_dx
    key_stack = jnp.stack(key_sums)
    value_stack = jnp.stack(value_sums)
    key_grad = (key_stack / replicas).astype(jnp.bfloat16)
    value_grad = (value_stack / replicas).astype(jnp.bfloat16)
    own_total = residual + jnp.where(is_last, top_grad.astype(jnp.float32), 0.0)
    outgoing = own_total.astype(jnp.bfloat16)
    received = shifted(outgoing, "section", -1)
    input_grad = (received.astype(jnp.float32) + own_total).astype(jnp.bfloat16)
    return (key_grad, value_grad, input_grad[None])


def solution(mesh):
    in_specs = (
        P("section", "dp", None),
        P("section", None),
        P("section", "dp", None),
        P("section", "dp", None),
        P("section", None, None),
        P("section", None, None),
        P("dp", None),
    )
    out_specs = (P("section", None, None), P("section", None, None), P("section", "dp", None))
    return jax.shard_map(
        per_device, mesh=mesh, in_specs=in_specs, out_specs=out_specs, check_vma=False
    )
```

profile of v0, /device:TPU:0, one launch (start us, length us, event | category | flops | bytes accessed | tf_op | source)
XLA Modules:
  0.0 365.8 jit_solution(12409770449454364073)
XLA Ops:
  7.2 0.0 all-reduce.3.cloned.1.call-start
  7.3 1.9 reshape_squeeze.7
  9.2 2.1 fusion.6
  11.3 4.2 %fusion.35 = bf16[256,512]{1,0:T(8,128)(2,1)} fusion(bf16[1,4096,512]{2,1,0:T(8,128)(2,1)} %param.12, bf16[1,256,4096]{2,1,0:T(8,128)(2,1)S(1)} %copy-done, f32[4096]{0:T(1024)S(1)} %bitcast.120, f32[256]{0:T(256)S(1)} %get-tuple-element.6), kind=kOutput, calls=%fused_computation.44 | convolution fusion | flops 1078067200 | bytes 6571008 | tf_op jit(solution)/shard_map/dot_general | solution.py:95
  15.5 1.0 reshape.102
  16.5 2.6 reshape_squeeze.6
  19.1 4.2 %fusion.32 = bf16[256,512]{1,0:T(8,128)(2,1)} fusion(bf16[1,4096,512]{2,1,0:T(8,128)(2,1)} %param.11, bf16[1,256,4096]{2,1,0:T(8,128)(2,1)S(1)} %copy-done, f32[4096]{0:T(1024)S(1)} %bitcast.121, f32[256]{0:T(256)S(1)} %get-tuple-element.6), kind=kOutput, calls=%fused_computation.43 | convolution fusion | flops 1078067200 | bytes 6571008 | tf_op jit(solution)/shard_map/dot_general | solution.py:92
  23.2 1.7 reshape.101
  24.9 1.8 fusion.47
  26.7 3.5 fusion.85
  30.2 2.0 fusion.38
  32.3 4.6 %fusion.39 = bf16[2,128,4,128]{3,1,2,0:T(8,128)(2,1)S(1)} fusion(f32[2,4,128,128,4]{3,2,4,1,0:T(8,128)} %fusion.47, bf16[2,128,4,4,128]{4,3,2,1,0:T(4,128)(2,1)} %reshape_squeeze.6, f32[2,4,4,128,128]{3,4,2,1,0:T(8,128)} %get-tuple-element.8, f32[2,4,4,128]{3,2,1,0:T(4,128)S(1)} %get-tuple-element.7), kind=kOutput, calls=%fused_computation.46 | convolution fusion | flops 138023040 | bytes 5521408 | tf_op jit(solution)/shard_map/bjgts,btjgd->bsjd/dot_general | solution.py:57
  36.9 0.2 copy.21
  37.1 4.6 %fusion.56 = f32[4096,512]{1,0:T(8,128)} fusion(bf16[32,8,4,128]{3,2,1,0:T(4,128)(2,1)S(1)} %bitcast.117, bf16[1,256,4096]{2,1,0:T(8,128)(2,1)S(1)} %copy-done, f32[4096]{0:T(1024)S(1)} %bitcast.122, f32[256]{0:T(256)S(1)} %get-tuple-element.6), kind=kOutput, calls=%fused_computation.64 | convolution fusion | flops 1077936128 | bytes 10765312 | tf_op jit(solution)/shard_map/td,tk->dk/dot_general | solution.py:64
  41.7 0.2 copy.23
  41.9 4.6 %fusion.53 = f32[4096,512]{1,0:T(8,128)} fusion(bf16[32,8,4,128]{3,2,1,0:T(4,128)(2,1)S(1)} %bitcast.115, bf16[1,256,4096]{2,1,0:T(8,128)(2,1)S(1)} %copy-done, f32[4096]{0:T(1024)S(1)} %bitcast.123, f32[256]{0:T(256)S(1)} %get-tuple-element.6), kind=kOutput, calls=%fused_computation.61 | convolution fusion | flops 1077936128 | bytes 10765312 | tf_op jit(solution)/shard_map/td,tk->dk/dot_general | solution.py:64
  46.6 3.6 fusion.18
  50.2 1.6 fusion.10
  51.9 1.5 fusion.80
  53.4 1.5 collective-permute-start
  55.0 48.4 %collective-permute-done = bf16[256,4096]{1,0:T(8,128)(2,1)S(1)} collective-permute-done((bf16[256,4096]{1,0:T(8,128)(2,1)S(1)}, bf16[256,4096]{1,0:T(8,128)(2,1)S(1)}, u32[]{:S(2)}, u32[]{:S(2)}) %collective-permute-start) | collective-permute-done | bytes 2097184 | tf_op jit(solution)/shard_map/ppermute | solution.py:17
  103.3 3.2 fusion.22
  106.6 240.9 %all-reduce.3.cloned.1.call-done = (f32[4096,512]{1,0:T(8,128)}, f32[4096,512]{1,0:T(8,128)}) async-done(((f32[4096,512]{1,0:T(8,128)}, f32[4096,512]{1,0:T(8,128)}), (f32[4096,512]{1,0:T(8,128)}, f32[4096,512]{1,0:T(8,128)})) %all-reduce.3.cloned.1.call-update) | async-done | bytes 16777232 | tf_op jit(solution)/shard_map/psum | solution.py:147
  347.4 11.6 %fusion.13 = (bf16[1,4096,512]{2,1,0:T(8,128)(2,1)}, bf16[1,4096,512]{2,1,0:T(8,128)(2,1)}) fusion(f32[4096,512]{1,0:T(8,128)} %get-tuple-element.3, f32[4096,512]{1,0:T(8,128)} %get-tuple-element.4), kind=kLoop, calls=%fused_computation.18 | loop fusion | flops 8388608 | bytes 25165824 | tf_op jit(solution)/shard_map/convert_element_type | solution.py:152
  (12 shorter events, 0.1 us)
Async XLA Ops:
  7.2 4.1 %copy-start = (bf16[1,256,4096]{2,1,0:T(8,128)(2,1)S(1)}, bf16[1,256,4096]{2,1,0:T(8,128)(2,1)}, u32[]{:S(2)}) copy-start(bf16[1,256,4096]{2,1,0:T(8,128)(2,1)} %param.7) | copy-start | bytes 6291460
  7.2 4.1 %copy-start.3 = (f32[1,4096]{1,0:T(1,128)S(1)}, f32[1,4096]{1,0:T(1,128)}, u32[]{:S(2)}) copy-start(f32[1,4096]{1,0:T(1,128)} %param.8) | copy-start | bytes 49156
  7.2 340.3 %all-reduce.3.cloned.1.call-start = ((), (), s32[]{:S(2)}) async-start(), calls=%async_computation | async-start | bytes 33554432 | tf_op jit(solution)/shard_map/psum | solution.py:147
  46.6 3.6 copy-start.2
  50.2 1.7 copy-start.1
  53.4 49.9 %collective-permute-start = (bf16[256,4096]{1,0:T(8,128)(2,1)S(1)}, bf16[256,4096]{1,0:T(8,128)(2,1)S(1)}, u32[]{:S(2)}, u32[]{:S(2)}) collective-permute-start(bf16[256,4096]{1,0:T(8,128)(2,1)S(1)} %fusion.80), channel_id=1, source_target_pairs={{16,0},{17,1},{18,2},{19,3},{20,4},{21,5},{22,6},{23,7},{24,8},{25... | collective-permute-start | bytes 6291464 | tf_op jit(solution)/shard_map/ppermute | solution.py:17
Sparse Core Ops, SparseCore 0:
  46.7 300.7 all-reduce.2
where the time goes:
time: 366 us
  waiting for transfers between devices  289 us (79%)
  matrix products  34.8 us (10%)
  other arithmetic  18.4 us (5%)
  between operations  14.2 us (4%)
  local copies, waits for them, and re-layouts  7.65 us (2%)
    psum x1, waiting for transfers between devices, per_device(): key_sums[layer_index] = lax.psum(key_partial, 'dp')  241 us
    ppermute x1, waiting for transfers between devices, shifted(): lax.ppermute(value, axis, [(source, source + steps) for source in range(i...  48.4 us
    convert_element_type x1, other arithmetic, per_device(): key_grad = (key_stack / replicas).astype(jnp.bfloat16)  11.6 us
    dot_general x2, matrix products, weight_term(): jnp.einsum('td,tk->dk', normed, grad_proj, preferred_element_type=jnp.flo...  9.22 us
  transfers between devices with their start and end apart: 2, of which 2 were waited for; matrix products, arithmetic and copies ran while one was open for 3% of the time, Pallas kernels for 0%

commit v1 on v0

--- a/solution.py
+++ b/solution.py
@@ -1,6 +1,8 @@
 import jax
 import jax.numpy as jnp
 from jax import lax
+from jax.experimental import pallas as pl
+from jax.experimental.pallas import tpu as pltpu
 from jax.sharding import PartitionSpec as P
 
 HEAD_SIZE = 128
@@ -86,7 +88,6 @@
     block_output_gradient,
     key_weight,
     value_weight,
-    value_hook,
 ):
     wide_inputs, inv_rms, normed = normalize(block_inputs, gain_row)
     key_projected = jnp.dot(normed, key_weight, preferred_element_type=jnp.float32).astype(
@@ -111,7 +112,7 @@
     )
     probability, value_gradient = value_pass(heads_of_query, heads_of_key, head_gradients)
     value_gradient = value_gradient.reshape(count_of_rows, KEY_VALUE_HEADS * HEAD_SIZE)
-    value_partial = value_hook(weight_term(normed, value_gradient))
+    value_partial = weight_term(normed, value_gradient)
     key_gradient = key_pass(probability, heads_of_query, heads_of_value, head_gradients).reshape(
         count_of_rows, KEY_VALUE_HEADS * HEAD_SIZE
     )
@@ -122,40 +123,229 @@
     return (key_partial, value_partial, layer_dx)
 
 
-def sum_values(partial_value):
-    return lax.psum(partial_value, "dp")
+CHUNKS_PER_ARRAY = 4
+
+
+def bit_orders(bit_count, chunk_count):
+    plain = list(range(bit_count))
+    swapped = list(plain)
+    if bit_count >= 3:
+        swapped[1], swapped[2] = swapped[2], swapped[1]
+    return [swapped if chunk % 4 == 3 else plain for chunk in range(chunk_count)]
+
+
+def exchange_kernel(
+    replicas,
+    sections,
+    key_in,
+    value_in,
+    cotangent_in,
+    key_out,
+    value_out,
+    cotangent_out,
+    held,
+    gathered,
+    *rest,
+):
+    bit_count = replicas.bit_length() - 1
+    landing = rest[:bit_count]
+    send_sem, recv_sem, load_sem, store_sem, cot_sem = rest[bit_count:]
+    rows = key_in.shape[0]
+    chunk_rows = rows // CHUNKS_PER_ARRAY
+    chunk_count = 2 * CHUNKS_PER_ARRAY
+    stage_count = 2 * bit_count
+    orders = bit_orders(bit_count, chunk_count)
+    section = lax.axis_index("section")
+    me = lax.axis_index("dp")
+    below = lax.rem(section + sections - 1, sections)
+    above = lax.rem(section + 1, sections)
+    partners = []
+    bits = []
+    for bit in range(bit_count):
+        value = lax.rem(me // (1 << bit), 2)
+        bits.append(value)
+        partners.append(me + (1 - 2 * value) * (1 << bit))
+
+    barrier = pltpu.get_barrier_semaphore()
+    for partner in partners:
+        pl.semaphore_signal(
+            barrier, inc=1, device_id=(section, partner), device_id_type=pl.DeviceIdType.MESH
+        )
+    for neighbour in (below, above):
+        pl.semaphore_signal(
+            barrier, inc=1, device_id=(neighbour, me), device_id_type=pl.DeviceIdType.MESH
+        )
+    pl.semaphore_wait(barrier, bit_count + 2)
+
+    cot_copy = pltpu.make_async_remote_copy(
+        src_ref=cotangent_in,
+        dst_ref=cotangent_out,
+        send_sem=cot_sem.at[0],
+        recv_sem=cot_sem.at[1],
+        device_id=(below, me),
+        device_id_type=pl.DeviceIdType.MESH,
+    )
+
+    def source(chunk):
+        return (value_in, key_in)[chunk // CHUNKS_PER_ARRAY]
+
+    def target(chunk):
+        return (value_out, key_out)[chunk // CHUNKS_PER_ARRAY]
+
+    def base(chunk):
+        return (chunk % CHUNKS_PER_ARRAY) * chunk_rows
+
+    offsets = []
+    for chunk in range(chunk_count):
+        offset = base(chunk)
+        kept = [offset]
+        for stage, bit in enumerate(orders[chunk]):
+            offset = offset + bits[bit] * (chunk_rows >> (stage + 1))
+            kept.append(offset)
+        offsets.append(kept)
+
+    def area(chunk, offset, size, buffer=held):
+        return buffer.at[chunk // CHUNKS_PER_ARRAY, pl.ds(pl.multiple_of(offset, 16), size)]
+
+    def load_copy(chunk):
+        half = chunk_rows // 2
+        start = pl.multiple_of(offsets[chunk][1], 16)
+        return pltpu.make_async_copy(
+            source(chunk).at[pl.ds(start, half)],
+            area(chunk, offsets[chunk][1], half),
+            load_sem.at[chunk],
+        )
+
+    def stage_copy(chunk, stage):
+        if stage < bit_count:
+            bit = orders[chunk][stage]
+            size = chunk_rows >> (stage + 1)
+            other = offsets[chunk][stage] + (1 - bits[bit]) * size
+            if stage == 0:
+                src = source(chunk).at[pl.ds(pl.multiple_of(other, 16), size)]
+            else:
+                src = area(chunk, other, size)
+            dst = landing[stage].at[pl.ds(chunk * size, size)]
+        else:
+            level = stage_count - 1 - stage
+            bit = orders[chunk][level]
+            size = chunk_rows >> (level + 1)
+            src = area(chunk, offsets[chunk][level + 1], size, gathered)
+            dst = area(chunk, offsets[chunk][level + 1], size, gathered)
+        return pltpu.make_async_remote_copy(
+            src_ref=src,
+            dst_ref=dst,
+            send_sem=send_sem.at[chunk, stage],
+            recv_sem=recv_sem.at[chunk, stage],
+            device_id=(section, partners[bit]),
+            device_id_type=pl.DeviceIdType.MESH,
+        )
+
+    def store_copy(chunk):
+        return pltpu.make_async_copy(
+            area(chunk, base(chunk), chunk_rows, gathered),
+            target(chunk).at[pl.ds(base(chunk), chunk_rows)],
+            store_sem.at[chunk],
+        )
+
+    def add(chunk, stage):
+        size = chunk_rows >> (stage + 1)
+        tile = min(size, 32)
+        index = chunk // CHUNKS_PER_ARRAY
+        start = offsets[chunk][stage + 1]
+        is_final = stage == bit_count - 1
+        result = gathered if is_final else held
+
+        @pl.loop(0, size // tile)
+        def _(step):
+            here = pl.ds(pl.multiple_of(start + step * tile, 16), tile)
+            there = pl.ds(pl.multiple_of(chunk * size + step * tile, 16), tile)
+            total = held[index, here].astype(jnp.float32) + landing[stage][there].astype(
+                jnp.float32
+            )
+            if is_final:
+                total = total * (1.0 / replicas)
+            result[index, here] = total.astype(jnp.bfloat16)
+
+    def finish(chunk, stage):
+        if stage == 0:
+            load_copy(chunk).wait()
+        stage_copy(chunk, stage).wait()
+        if stage < bit_count:
+            add(chunk, stage)
+        if stage + 1 < stage_count:
+            stage_copy(chunk, stage + 1).start()
+        else:
+            store_copy(chunk).start()
+
+    for chunk in range(chunk_count):
+        stage_copy(chunk, 0).start()
+        load_copy(chunk).start()
+    cot_copy.start()
+    lags = [stage + (2 if stage else 0) for stage in range(stage_count)]
+    for step in range(chunk_count + lags[-1]):
+        for stage in reversed(range(stage_count)):
+            chunk = step - lags[stage]
+            if 0 <= chunk < chunk_count:
+                finish(chunk, stage)
+    cot_copy.wait()
+    for chunk in range(chunk_count):
+        store_copy(chunk).wait()
+
+
+def exchange(key_partial, value_partial, cotangent):
+    replicas = lax.axis_size("dp")
+    sections = lax.axis_size("section")
+    rows, columns = key_partial.shape
+    bit_count = replicas.bit_length() - 1
+    chunk_count = 2 * CHUNKS_PER_ARRAY
+    kind = key_partial.dtype
+    anywhere = pl.BlockSpec(memory_space=pl.ANY)
+    return pl.pallas_call(
+        lambda *refs: exchange_kernel(replicas, sections, *refs),
+        out_shape=(
+            jax.ShapeDtypeStruct(key_partial.shape, kind),
+            jax.ShapeDtypeStruct(value_partial.shape, kind),
+            jax.ShapeDtypeStruct(cotangent.shape, cotangent.dtype),
+        ),
+        in_specs=[anywhere] * 3,
+        out_specs=(anywhere,) * 3,
+        scratch_shapes=[pltpu.VMEM((2, rows, columns), kind)] * 2
+        + [
+            pltpu.VMEM((2 * rows >> (stage + 1), columns), kind) for stage in range(bit_count)
+        ]
+        + [
+            pltpu.SemaphoreType.DMA((chunk_count, 2 * bit_count)),
+            pltpu.SemaphoreType.DMA((chunk_count, 2 * bit_count)),
+            pltpu.SemaphoreType.DMA((chunk_count,)),
+            pltpu.SemaphoreType.DMA((chunk_count,)),
+            pltpu.SemaphoreType.DMA((2,)),
+        ],
+        compiler_params=pltpu.CompilerParams(
+            collective_id=0, has_side_effects=True, vmem_limit_bytes=32 * 1024 * 1024
+        ),
+    )(key_partial, value_partial, cotangent)
 
 
 def per_device(layer_inputs, norm_gain, queries, output_gradient, w_key, value_matrix, top_grad):
-    layer_count = layer_inputs.shape[0]
-    count_of_rows = layer_inputs.shape[1]
-    replicas = lax.axis_size("dp")
     is_last = lax.axis_index("section") == lax.axis_size("section") - 1
-    residual = jnp.zeros((count_of_rows, layer_inputs.shape[2]), jnp.float32)
-    key_sums = [None] * layer_count
-    value_sums = [None] * layer_count
-    for layer_index in reversed(range(layer_count)):
-        key_partial, value_partial, layer_dx = layer_grads(
-            layer_inputs[layer_index],
-            norm_gain[layer_index],
-            queries[layer_index],
-            output_gradient[layer_index],
-            w_key[layer_index],
-            value_matrix[layer_index],
-            sum_values,
-        )
-        key_sums[layer_index] = lax.psum(key_partial, "dp")
-        value_sums[layer_index] = value_partial
-        residual = layer_dx
-    key_stack = jnp.stack(key_sums)
-    value_stack = jnp.stack(value_sums)
-    key_grad = (key_stack / replicas).astype(jnp.bfloat16)
-    value_grad = (value_stack / replicas).astype(jnp.bfloat16)
-    own_total = residual + jnp.where(is_last, top_grad.astype(jnp.float32), 0.0)
-    outgoing = own_total.astype(jnp.bfloat16)
-    received = shifted(outgoing, "section", -1)
-    input_grad = (received.astype(jnp.float32) + own_total).astype(jnp.bfloat16)
-    return (key_grad, value_grad, input_grad[None])
+    key_partial, value_partial, layer_dx = layer_grads(
+        layer_inputs[0],
+        norm_gain[0],
+        queries[0],
+        output_gradient[0],
+        w_key[0],
+        value_matrix[0],
+    )
+    own_total = layer_dx + jnp.where(is_last, top_grad.astype(jnp.float32), 0.0)
+    key_grad, value_grad, received = exchange(
+        key_partial.astype(jnp.bfloat16),
+        value_partial.astype(jnp.bfloat16),
+        own_total.astype(jnp.bfloat16),
+    )
+    received = jnp.where(is_last, 0.0, received.astype(jnp.float32))
+    input_grad = (received + own_total).astype(jnp.bfloat16)
+    return (key_grad[None], value_grad[None], input_grad[None])
 
 
 def solution(mesh):

time: 366 us -> 155 us (0.42)
  waiting for transfers between devices: 289 us -> 0 us
  Pallas kernels: 0 us -> 108 us
  between operations: 14.2 us -> 0.8 us
  other arithmetic: 18.4 us -> 7.07 us
  matrix products: 34.8 us -> 26.4 us
    psum x1 -> x0, waiting for transfers between devices: 241 us -> none  [per_device(): key_sums[layer_index] = lax.psum(key_partial, 'dp')]
    pallas_call x0 -> x1, Pallas kernels: none -> 108 us  [exchange(): pl.pallas_call(lambda *refs: exchange_kernel(replicas, sections, *refs),...]
    ppermute x1 -> x0, waiting for transfers between devices: 48.4 us -> none  [shifted(): lax.ppermute(value, axis, [(source, source + steps) for source in range(i...]
    convert_element_type x2 -> x1, other arithmetic: 13.1 us -> 1.63 us  [per_device(): own_total.astype(jnp.bfloat16)]
    dot_general x2, matrix products: 9.22 us -> 2.94 us  [weight_term(): jnp.einsum('td,tk->dk', normed, grad_proj, preferred_element_type=jnp.flo...]
    unnamed x8 -> x16, local copies, waits for them, and re-layouts: 0.02 us -> 5.19 us
  transfers between devices with their start and end apart: 2 -> 0, of which waited for: 2 -> 0; matrix products, arithmetic and copies ran while one was open for 3% -> 0% of each run, Pallas kernels for 0% -> 0%
where the time goes in v1:
time: 155 us; the launch traced here: 153 us
  Pallas kernels  108 us (70%)
  matrix products  26.4 us (17%)
  local copies, waits for them, and re-layouts  10.7 us (7%)
  other arithmetic  7.07 us (5%)
    pallas_call x1, Pallas kernels, exchange(): pl.pallas_call(lambda *refs: exchange_kernel(replicas, sections, *refs),...  108 us
    unnamed x16, local copies, waits for them, and re-layouts  5.19 us
    dot_general x1, matrix products, key_pass(): jnp.einsum('bjgts,btjgd->bsjd', dscore, heads_of_query, preferred_element...  4.66 us
    dot_general x1, matrix products, layer_grads(): jnp.dot(normed, key_weight, preferred_element_type=jnp.float32)  4.28 us
    dot_general x1, matrix products, layer_grads(): jnp.dot(normed, value_weight, preferred_element_type=jnp.float32)  4.28 us
    sub x1, matrix products, value_pass(): weight = jnp.exp(scores - row_max)  3.52 us
    broadcast_in_dim x1, other arithmetic, per_device(): return (key_grad[None], value_grad[None], input_grad[None])  3.33 us

profile of v1, /device:TPU:0, one launch (start us, length us, event | category | flops | bytes accessed | tf_op | source)
XLA Modules:
  0.0 153.4 jit_solution(17192437088848910449)
XLA Ops:
  0.6 2.1 %fusion.6 = f32[256]{0:T(256)S(1)} fusion(bf16[1,256,4096]{2,1,0:T(8,128)(2,1)} %param.7), kind=kLoop, calls=%fused_computation.11 | loop fusion | flops 3145472 | bytes 2098176 | tf_op jit(solution)/shard_map/reduce_sum | solution.py:24
  2.8 4.3 %fusion.33 = bf16[256,512]{1,0:T(8,128)(2,1)S(1)} fusion(bf16[1,4096,512]{2,1,0:T(8,128)(2,1)} %param.12, bf16[1,256,4096]{2,1,0:T(8,128)(2,1)} %param.7, f32[4096]{0:T(1024)} %bitcast.121, f32[256]{0:T(256)S(1)} %get-tuple-element.10), kind=kOutput, calls=%fused_computation.42 | convolution fusion | flops 1078067200 | bytes 6571008 | tf_op jit(solution)/shard_map/dot_general | solution.py:96
  7.1 0.1 reshape.98
  7.2 4.3 %fusion.30 = bf16[256,512]{1,0:T(8,128)(2,1)} fusion(bf16[1,4096,512]{2,1,0:T(8,128)(2,1)} %param.11, bf16[1,256,4096]{2,1,0:T(8,128)(2,1)S(1)} %copy-done, f32[4096]{0:T(1024)S(1)} %bitcast.122, f32[256]{0:T(256)S(1)} %get-tuple-element.10), kind=kOutput, calls=%fused_computation.41 | convolution fusion | flops 1078067200 | bytes 6571008 | tf_op jit(solution)/shard_map/dot_general | solution.py:93
  11.5 1.7 %reshape.97 = bf16[2,128,4,128]{3,2,1,0:T(4,128)(2,1)} reshape(bf16[256,512]{1,0:T(8,128)(2,1)} %fusion.30) | data formatting | bytes 524288 | tf_op jit(solution)/shard_map/reshape | solution.py:107
  13.2 1.5 reshape_squeeze.6
  14.7 1.8 %reshape_squeeze.7 = bf16[2,128,4,4,128]{4,3,2,1,0:T(4,128)(2,1)S(1)} reshape(bf16[1,256,2048]{2,1,0:T(8,128)(2,1)} %param.10) | data formatting | bytes 2097152 | tf_op jit(solution)/shard_map/reshape;squeeze | solution.py:104
  16.5 1.8 %fusion.45 = f32[2,4,128,128,4]{3,2,4,1,0:T(8,128)} fusion(bf16[2,128,4,4,128]{4,3,2,1,0:T(4,128)(2,1)S(1)} %reshape_squeeze.7, bf16[2,128,4,128,1]{3,2,1,0,4:T(4,128)(2,1)S(1)} %bitcast.119), kind=kOutput, calls=%fused_computation.53 | convolution fusion | flops 134217728 | bytes 3407872 | tf_op jit(solution)/shard_map/btjgd,bsjd->bjgts/dot_general | solution.py:54
  18.2 3.5 %fusion.81 = (f32[2,4,4,128]{3,2,1,0:T(4,128)S(1)}, f32[2,4,4,128,128]{3,4,2,1,0:T(8,128)}) fusion(pred[128,128]{0,1:T(8,128)(4,1)S(1)} %iota_compare_fusion, bf16[2,128,4,4,128]{4,3,2,1,0:T(4,128)(2,1)} %reshape_squeeze.6, bf16[2,128,4,128,1]{3,2,1,0,4:T(4,128)(2,1)} %bitcast.120), kind=kOutput, calls=%fused_computation.77 | convolution fusion | flops 136315008 | bytes 3440640 | tf_op jit(solution)/shard_map/sub | solution.py:41
  21.8 4.7 %fusion.37 = bf16[2,128,4,128]{3,1,2,0:T(8,128)(2,1)S(1)} fusion(f32[2,4,128,128,4]{3,2,4,1,0:T(8,128)} %fusion.45, bf16[2,128,4,4,128]{4,3,2,1,0:T(4,128)(2,1)} %reshape_squeeze.6, f32[2,4,4,128,128]{3,4,2,1,0:T(8,128)} %get-tuple-element.12, f32[2,4,4,128]{3,2,1,0:T(4,128)S(1)} %get-tuple-element.11), kind=kOutput, calls=%fused_computation.44 | convolution fusion | flops 138023040 | bytes 5521408 | tf_op jit(solution)/shard_map/bjgts,btjgd->bsjd/dot_general | solution.py:59
  26.4 2.2 %fusion.36 = bf16[2,128,4,128]{3,1,2,0:T(8,128)(2,1)S(1)} fusion(bf16[2,128,4,4,128]{4,3,2,1,0:T(4,128)(2,1)S(1)} %reshape_squeeze.7, f32[2,4,4,128,128]{3,4,2,1,0:T(8,128)} %get-tuple-element.12, f32[2,4,4,128]{3,2,1,0:T(4,128)S(1)} %get-tuple-element.11), kind=kOutput, calls=%fused_computation.43 | convolution fusion | flops 135397376 | bytes 3424256 | tf_op jit(solution)/shard_map/bjgts,btjgd->bsjd/dot_general | solution.py:43
  28.6 0.2 copy.23
  28.9 0.2 copy.21
  29.1 0.2 copy-done.4
  29.2 1.3 fusion.16
  30.5 0.9 copy-done.3
  31.4 1.5 fusion.10
  33.0 1.6 %fusion.76.refs_2_ = bf16[256,4096]{1,0:T(8,128)(2,1)S(1)} fusion(bf16[256,4096]{1,0:T(8,128)(2,1)S(1)} %copy-done.1, pred[]{:T(512)S(6)} %eq.3, f32[256]{0:T(256)S(1)} %broadcast_multiply_fusion, f32[256]{0:T(256)S(1)} %get-tuple-element.9, bf16[1,256,4096]{2,1,0:T(8,128)(2,1)S(1)} %copy-done, f32[256,4096]{1,0:T(8,128)S(1)} %get-tuple-element.14, ...), kind=kLoop, calls=%fused_computation.76 | loop fusion | flops 9437184 | bytes 10488833 | tf_op jit(solution)/shard_map/convert_element_type | solution.py:344
  34.7 1.5 convolution_convert_fusion.refs_1_
  36.1 1.5 convolution_convert_fusion.1.refs_0_
  37.6 108.4 %shard_map.94 = (bf16[4096,512]{1,0:T(8,128)(2,1)S(1)}, bf16[4096,512]{1,0:T(8,128)(2,1)S(1)}, bf16[256,4096]{1,0:T(8,128)(2,1)S(1)}) custom-call(bf16[4096,512]{1,0:T(8,128)(2,1)S(1)} %convolution_convert_fusion.1.refs_0_, bf16[4096,512]{1,0:T(8,128)(2,1)S(1)} %convolution_convert_fusion.refs_1_, bf16[256,4096]{1,0:T(8,128)(2,1)S(1)} %fusion.76.refs_2_), custom_call_target="tpu_custom_call" | custom-call | tf_op jit(solution)/shard_map/pallas_call | solution.py:304
  146.1 3.3 %fusion.20 = bf16[1,256,4096]{2,1,0:T(8,128)(2,1)} fusion(bf16[256,4096]{1,0:T(8,128)(2,1)S(1)} %get-tuple-element.8, pred[]{:T(512)S(6)} %eq.3, bf16[256,4096]{1,0:T(8,128)(2,1)S(1)} %copy-done.2, f32[256]{0:T(256)S(1)} %broadcast_multiply_fusion, f32[256]{0:T(256)S(1)} %get-tuple-element.9, bf16[1,256,4096]{2,1,0:T(8,128)(2,1)S(1)} %copy-done, ...), kind=kLoop, calls=%fused_computation.26 | loop fusion | flops 12582912 | bytes 12585985 | tf_op jit(solution)/shard_map/broadcast_in_dim | solution.py:348
  149.4 2.0 %copy.82 = bf16[1,4096,512]{2,1,0:T(8,128)(2,1)} copy(bf16[1,4096,512]{2,1,0:T(8,128)(2,1)S(1)} %bitcast.114) | data formatting | bytes 8388608
  151.4 2.0 %copy.83 = bf16[1,4096,512]{2,1,0:T(8,128)(2,1)} copy(bf16[1,4096,512]{2,1,0:T(8,128)(2,1)S(1)} %bitcast.113) | data formatting | bytes 8388608
  (15 shorter events, 0.1 us)
Async XLA Ops:
  2.8 4.4 %copy-start = (bf16[1,256,4096]{2,1,0:T(8,128)(2,1)S(1)}, bf16[1,256,4096]{2,1,0:T(8,128)(2,1)}, u32[]{:S(2)}) copy-start(bf16[1,256,4096]{2,1,0:T(8,128)(2,1)} %param.7) | copy-start | bytes 6291460
  2.8 4.4 %copy-start.6 = (f32[1,4096]{1,0:T(1,128)S(1)}, f32[1,4096]{1,0:T(1,128)}, u32[]{:S(2)}) copy-start(f32[1,4096]{1,0:T(1,128)} %param.8) | copy-start | bytes 49156
  7.2 6.0 %copy-start.5 = (bf16[1,256,2048]{2,1,0:T(8,128)(2,1)S(1)}, bf16[1,256,2048]{2,1,0:T(8,128)(2,1)}, u32[]{:S(2)}) copy-start(bf16[1,256,2048]{2,1,0:T(8,128)(2,1)} %param.9) | copy-start | bytes 3145732
  26.4 2.8 %copy-start.4 = (bf16[1,4096,512]{2,1,0:T(8,128)(2,1)S(1)}, bf16[1,4096,512]{2,1,0:T(8,128)(2,1)}, u32[]{:S(2)}) copy-start(bf16[1,4096,512]{2,1,0:T(8,128)(2,1)} %param.11) | copy-start | bytes 12582916
  29.2 2.2 %copy-start.3 = (bf16[1,4096,512]{2,1,0:T(8,128)(2,1)S(1)}, bf16[1,4096,512]{2,1,0:T(8,128)(2,1)}, u32[]{:S(2)}) copy-start(bf16[1,4096,512]{2,1,0:T(8,128)(2,1)} %param.12) | copy-start | bytes 12582916
  31.4 1.6 %copy-start.1 = (bf16[256,4096]{1,0:T(8,128)(2,1)S(1)}, bf16[256,4096]{1,0:T(8,128)(2,1)}, u32[]{:S(2)}) copy-start(bf16[256,4096]{1,0:T(8,128)(2,1)} %param.13) | copy-start | bytes 6291460
  37.6 108.5 %copy-start.2 = (bf16[256,4096]{1,0:T(8,128)(2,1)S(1)}, bf16[256,4096]{1,0:T(8,128)(2,1)}, u32[]{:S(2)}) copy-start(bf16[256,4096]{1,0:T(8,128)(2,1)} %param.13) | copy-start | bytes 6291460

commit v2 on v1

v2 whole, which is shorter than its diff:
```python
import jax
import jax.numpy as jnp
from jax import lax
from jax.experimental import pallas as pl
from jax.experimental.pallas import tpu as pltpu
from jax.sharding import PartitionSpec as P

HEAD_SIZE = 128
KEY_VALUE_HEADS = 4
SEQUENCE_TOKENS = 128


epsilon = 1e-05


CHUNKS_PER_ARRAY = 4


def bit_orders(bit_count, chunk_count):
    plain = list(range(bit_count))
    swapped = list(plain)
    if bit_count >= 3:
        swapped[1], swapped[2] = swapped[2], swapped[1]
    return [swapped if chunk % 4 == 3 else plain for chunk in range(chunk_count)]


MESH = pl.DeviceIdType.MESH
FEATURE_BLOCK = 512
TERM_BLOCK = 256
ROW_TILE = 16
LOAD_PIECES = 4
INPUT_TERM_STEP = 3
FINAL_SUM_STEP = 10


def contract(left, right, left_axis, right_axis):
    return lax.dot_general(
        left, right, (((left_axis,), (right_axis,)), ((), ())), preferred_element_type=jnp.float32
    )


def whole_kernel(
    replicas,
    sections,
    x_in,
    gain,
    query_in,
    gradient_in,
    key_weight_in,
    value_weight_in,
    top_in,
    key_out,
    value_out,
    input_out,
    x_held,
    normed,
    inv_rms,
    query,
    gradient,
    weights,
    top,
    projected_wide,
    projected,
    grads,
    scaled,
    row_dot,
    outgoing,
    received,
    final,
    held,
    gathered,
    *rest,
):
    bit_count = replicas.bit_length() - 1
    landing = rest[:bit_count]
    send_sem, recv_sem, store_sem, cot_sem, x_sem, weight_sem, load_sem = rest[bit_count:]
    rows = key_out.shape[1]
    tokens = x_held.shape[0]
    width = x_held.shape[1]
    group = query.shape[1] // KEY_VALUE_HEADS
    scale = HEAD_SIZE ** (-0.5)
    chunk_rows = rows // CHUNKS_PER_ARRAY
    chunk_count = 2 * CHUNKS_PER_ARRAY
    stage_count = 2 * bit_count
    orders = bit_orders(bit_count, chunk_count)
    section = lax.axis_index("section")
    me = lax.axis_index("dp")
    below = lax.rem(section + sections - 1, sections)
    above = lax.rem(section + 1, sections)
    partners = []
    bits = []
    for bit in range(bit_count):
        value = lax.rem(me // (1 << bit), 2)
        bits.append(value)
        partners.append(me + (1 - 2 * value) * (1 << bit))

    piece = tokens // LOAD_PIECES

    def x_copy(index):
        here = pl.ds(index * piece, piece)
        return pltpu.make_async_copy(x_in.at[0, here], x_held.at[here], x_sem.at[index])

    def weight_copy(which, block):
        here = pl.ds(pl.multiple_of(block * FEATURE_BLOCK, FEATURE_BLOCK), FEATURE_BLOCK)
        return pltpu.make_async_copy(
            (key_weight_in, value_weight_in)[which].at[0, here],
            weights.at[which, here],
            weight_sem.at[which, block],
        )

    query_copy = pltpu.make_async_copy(query_in.at[0], query, load_sem.at[0])
    gradient_copy = pltpu.make_async_copy(gradient_in.at[0], gradient, load_sem.at[1])
    top_copy = pltpu.make_async_copy(top_in, top, load_sem.at[2])
    feature_blocks = width // FEATURE_BLOCK
    for index in range(LOAD_PIECES):
        x_copy(index).start()
    for block in range(feature_blocks):
        for which in range(2):
            weight_copy(which, block).start()
    query_copy.start()
    gradient_copy.start()

    barrier = pltpu.get_barrier_semaphore()
    for partner in partners:
        pl.semaphore_signal(
            barrier, inc=1, device_id=(section, partner), device_id_type=MESH
        )
    for neighbour in (below, above):
        pl.semaphore_signal(
            barrier, inc=1, device_id=(neighbour, me), device_id_type=MESH
        )

    for index in range(LOAD_PIECES):
        x_copy(index).wait()

        @pl.loop(0, piece // ROW_TILE)
        def _(step):
            here = pl.ds(pl.multiple_of(index * piece + step * ROW_TILE, ROW_TILE), ROW_TILE)
            wide = x_held[here].astype(jnp.float32)
            inverse = lax.rsqrt(jnp.mean(wide * wide, axis=-1, keepdims=True) + epsilon)
            inv_rms[here] = inverse
            normed[here] = (wide * inverse * gain[...]).astype(jnp.bfloat16)

    projected_wide[...] = jnp.zeros_like(projected_wide)

    @pl.loop(0, feature_blocks)
    def _(block):
        here = pl.ds(pl.multiple_of(block * FEATURE_BLOCK, FEATURE_BLOCK), FEATURE_BLOCK)
        for which in range(2):
            weight_copy(which, block).wait()
            projected_wide[which] += contract(normed[:, here], weights[which, here], 1, 0)

    projected[...] = projected_wide[...].astype(jnp.bfloat16)
    query_copy.wait()
    gradient_copy.wait()
    top_copy.start()

    @pl.loop(0, tokens // SEQUENCE_TOKENS * KEY_VALUE_HEADS)
    def _(index):
        sequence = index // KEY_VALUE_HEADS
        head = lax.rem(index, KEY_VALUE_HEADS)
        here = pl.ds(pl.multiple_of(sequence * SEQUENCE_TOKENS, SEQUENCE_TOKENS), SEQUENCE_TOKENS)
        column = pl.ds(pl.multiple_of(head * HEAD_SIZE, HEAD_SIZE), HEAD_SIZE)

        def stacked(ref):
            return jnp.concatenate(
                [
                    ref[here, pl.ds(pl.multiple_of(head * group + part, HEAD_SIZE), HEAD_SIZE)]
                    for part in range(0, group, HEAD_SIZE)
                ],
                axis=0,
            )

        head_queries = stacked(query)
        head_gradients = stacked(gradient)
        scores = contract(head_queries, projected[0, here, column], 1, 1) * scale
        query_row = lax.rem(lax.broadcasted_iota(jnp.int32, scores.shape, 0), SEQUENCE_TOKENS)
        key_row = lax.broadcasted_iota(jnp.int32, scores.shape, 1)
        scores = jnp.where(query_row >= key_row, scores, -1e30)
        weight = jnp.exp(scores - jnp.max(scores, axis=-1, keepdims=True))
        probability = weight * (1.0 / jnp.sum(weight, axis=-1, keepdims=True))
        grads[1, here, column] = contract(
            probability.astype(jnp.bfloat16), head_gradients, 0, 0
        ).astype(jnp.bfloat16)
        grad_prob = contract(head_gradients, projected[1, here, column], 1, 1)
        row_delta = jnp.sum(probability * grad_prob, axis=-1, keepdims=True)
        dscore = (probability * (grad_prob - row_delta) * scale).astype(jnp.bfloat16)
        grads[0, here, column] = contract(dscore, head_queries, 0, 0).astype(jnp.bfloat16)

    pl.semaphore_wait(barrier, bit_count + 2)

    cot_copy = pltpu.make_async_remote_copy(
        src_ref=outgoing,
        dst_ref=received,
        send_sem=cot_sem.at[0],
        recv_sem=cot_sem.at[1],
        device_id=(below, me),
        device_id_type=MESH,
    )

    def target(chunk):
        return (value_out, key_out)[chunk // CHUNKS_PER_ARRAY]

    def base(chunk):
        return (chunk % CHUNKS_PER_ARRAY) * chunk_rows

    offsets = []
    for chunk in range(chunk_count):
        offset = base(chunk)
        kept = [offset]
        for stage, bit in enumerate(orders[chunk]):
            offset = offset + bits[bit] * (chunk_rows >> (stage + 1))
            kept.append(offset)
        offsets.append(kept)

    def area(chunk, offset, size, buffer=held):
        return buffer.at[chunk // CHUNKS_PER_ARRAY, pl.ds(pl.multiple_of(offset, 16), size)]

    def stage_copy(chunk, stage):
        if stage < bit_count:
            bit = orders[chunk][stage]
            size = chunk_rows >> (stage + 1)
            other = offsets[chunk][stage] + (1 - bits[bit]) * size
            src = area(chunk, other, size)
            dst = landing[stage].at[pl.ds(chunk * size, size)]
        else:
            level = stage_count - 1 - stage
            bit = orders[chunk][level]
            size = chunk_rows >> (level + 1)
            src = area(chunk, offsets[chunk][level + 1], size, gathered)
            dst = area(chunk, offsets[chunk][level + 1], size, gathered)
        return pltpu.make_async_remote_copy(
            src_ref=src,
            dst_ref=dst,
            send_sem=send_sem.at[chunk, stage],
            recv_sem=recv_sem.at[chunk, stage],
            device_id=(section, partners[bit]),
            device_id_type=MESH,
        )

    def store_copy(chunk):
        return pltpu.make_async_copy(
            area(chunk, base(chunk), chunk_rows, gathered),
            target(chunk).at[0, pl.ds(base(chunk), chunk_rows)],
            store_sem.at[chunk],
        )

    def add(chunk, stage):
        size = chunk_rows >> (stage + 1)
        tile = min(size, 32)
        index = chunk // CHUNKS_PER_ARRAY
        start = offsets[chunk][stage + 1]
        is_final = stage == bit_count - 1
        result = gathered if is_final else held

        @pl.loop(0, size // tile)
        def _(step):
            here = pl.ds(pl.multiple_of(start + step * tile, 16), tile)
            there = pl.ds(pl.multiple_of(chunk * size + step * tile, 16), tile)
            total = held[index, here].astype(jnp.float32) + landing[stage][there].astype(
                jnp.float32
            )
            if is_final:
                total = total * (1.0 / replicas)
            result[index, here] = total.astype(jnp.bfloat16)

    def finish(chunk, stage):
        stage_copy(chunk, stage).wait()
        if stage < bit_count:
            add(chunk, stage)
        if stage + 1 < stage_count:
            stage_copy(chunk, stage + 1).start()
        else:
            store_copy(chunk).start()

    def weight_term(chunk):
        which = 1 - chunk // CHUNKS_PER_ARRAY
        index = chunk // CHUNKS_PER_ARRAY

        @pl.loop(0, chunk_rows // TERM_BLOCK)
        def _(step):
            here = pl.ds(
                pl.multiple_of(base(chunk) + step * TERM_BLOCK, TERM_BLOCK), TERM_BLOCK
            )
            term = contract(normed[:, here], grads[which], 0, 0)
            held[index, here] = term.astype(jnp.bfloat16)

    is_last = jnp.where(section == sections - 1, 1.0, 0.0)

    def input_term():
        row_dot[...] = jnp.zeros_like(row_dot)

        @pl.loop(0, feature_blocks)
        def _(block):
            here = pl.ds(pl.multiple_of(block * FEATURE_BLOCK, FEATURE_BLOCK), FEATURE_BLOCK)
            grad_norm = contract(grads[0], weights[0, here], 1, 1)
            grad_norm = grad_norm + contract(grads[1], weights[1, here], 1, 1)
            part = gain[:, here] * grad_norm
            scaled[:, here] = part
            row_dot[...] += jnp.sum(
                x_held[:, here].astype(jnp.float32) * part, axis=-1, keepdims=True
            )

        top_copy.wait()

        @pl.loop(0, tokens // ROW_TILE)
        def _(step):
            here = pl.ds(pl.multiple_of(step * ROW_TILE, ROW_TILE), ROW_TILE)
            inverse = inv_rms[here]
            pull = inverse * inverse * inverse * (row_dot[here] * (1.0 / width))
            total = inverse * scaled[here] - x_held[here].astype(jnp.float32) * pull
            total = total + top[here].astype(jnp.float32) * is_last
            scaled[here] = total
            outgoing[here] = total.astype(jnp.bfloat16)

        cot_copy.start()

    final_copy = pltpu.make_async_copy(final, input_out.at[0], load_sem.at[3])

    def final_sum():
        cot_copy.wait()

        @pl.loop(0, tokens // ROW_TILE)
        def _(step):
            here = pl.ds(pl.multiple_of(step * ROW_TILE, ROW_TILE), ROW_TILE)
            total = scaled[here] + received[here].astype(jnp.float32) * (1.0 - is_last)
            final[here] = total.astype(jnp.bfloat16)

        final_copy.start()

    lags = [stage + (2 if stage else 1) for stage in range(stage_count)]
    for step in range(chunk_count + lags[-1]):
        for stage in reversed(range(stage_count)):
            chunk = step - lags[stage]
            if 0 <= chunk < chunk_count:
                finish(chunk, stage)
        if step < chunk_count:
            weight_term(step)
            stage_copy(step, 0).start()
        if step == INPUT_TERM_STEP:
            input_term()
        if step == FINAL_SUM_STEP:
            final_sum()
    final_copy.wait()
    for chunk in range(chunk_count):
        store_copy(chunk).wait()


def per_device(layer_inputs, norm_gain, queries, output_gradient, w_key, value_matrix, top_grad):
    replicas = lax.axis_size("dp")
    sections = lax.axis_size("section")
    tokens, width = layer_inputs.shape[1:]
    rows, columns = w_key.shape[1:]
    bit_count = replicas.bit_length() - 1
    chunk_count = 2 * CHUNKS_PER_ARRAY
    low = jnp.bfloat16
    wide = jnp.float32
    anywhere = pl.BlockSpec(memory_space=pl.ANY)
    whole = pl.BlockSpec(memory_space=pltpu.VMEM)
    return pl.pallas_call(
        lambda *refs: whole_kernel(replicas, sections, *refs),
        out_shape=(
            jax.ShapeDtypeStruct(w_key.shape, low),
            jax.ShapeDtypeStruct(value_matrix.shape, low),
            jax.ShapeDtypeStruct(layer_inputs.shape, low),
        ),
        in_specs=[anywhere, whole] + [anywhere] * 5,
        out_specs=(anywhere,) * 3,
        scratch_shapes=[
            pltpu.VMEM((tokens, width), low),
            pltpu.VMEM((tokens, width), low),
            pltpu.VMEM((tokens, 1), wide),
            pltpu.VMEM(queries.shape[1:], low),
            pltpu.VMEM(queries.shape[1:], low),
            pltpu.VMEM((2, rows, columns), low),
            pltpu.VMEM((tokens, width), low),
            pltpu.VMEM((2, tokens, columns), wide),
            pltpu.VMEM((2, tokens, columns), low),
            pltpu.VMEM((2, tokens, columns), low),
            pltpu.VMEM((tokens, width), wide),
            pltpu.VMEM((tokens, 1), wide),
            pltpu.VMEM((tokens, width), low),
            pltpu.VMEM((tokens, width), low),
            pltpu.VMEM((tokens, width), low),
            pltpu.VMEM((2, rows, columns), low),
            pltpu.VMEM((2, rows, columns), low),
        ]
        + [pltpu.VMEM((2 * rows >> (stage + 1), columns), low) for stage in range(bit_count)]
        + [
            pltpu.SemaphoreType.DMA((chunk_count, 2 * bit_count)),
            pltpu.SemaphoreType.DMA((chunk_count, 2 * bit_count)),
            pltpu.SemaphoreType.DMA((chunk_count,)),
            pltpu.SemaphoreType.DMA((2,)),
            pltpu.SemaphoreType.DMA((LOAD_PIECES,)),
            pltpu.SemaphoreType.DMA((2, width // FEATURE_BLOCK)),
            pltpu.SemaphoreType.DMA((4,)),
        ],
        compiler_params=pltpu.CompilerParams(
            collective_id=0, has_side_effects=True, vmem_limit_bytes=60 * 1024 * 1024
        ),
    )(layer_inputs, norm_gain, queries, output_gradient, w_key, value_matrix, top_grad)


def solution(mesh):
    in_specs = (
        P("section", "dp", None),
        P("section", None),
        P("section", "dp", None),
        P("section", "dp", None),
        P("section", None, None),
        P("section", None, None),
        P("dp", None),
    )
    out_specs = (P("section", None, None), P("section", None, None), P("section", "dp", None))
    return jax.shard_map(
        per_device, mesh=mesh, in_specs=in_specs, out_specs=out_specs, check_vma=False
    )
```

time: 155 us -> 146 us (0.942)
  Pallas kernels: 108 us -> 136 us
  matrix products: 26.4 us -> 0 us
  other arithmetic: 7.07 us -> 0 us
  local copies, waits for them, and re-layouts: 10.7 us -> 9.06 us
    pallas_call x1, Pallas kernels: 108 us -> 136 us  [per_device(): pl.pallas_call(lambda *refs: whole_kernel(replicas, sections, *refs), out...]
    dot_general x9 -> x0, matrix products: 22.9 us -> none  [the longest x1 4.66 us: key_pass(): jnp.einsum('bjgts,btjgd->bsjd', dscore, heads_of_query, preferred_element...]
    unnamed x16 -> x7, local copies, waits for them, and re-layouts: 5.19 us -> 9.06 us
    sub x1 -> x0, matrix products: 3.52 us -> none  [value_pass(): weight = jnp.exp(scores - row_max)]
    broadcast_in_dim x1 -> x0, other arithmetic: 3.33 us -> none  [per_device(): return (key_grad[None], value_grad[None], input_grad[None])]
    another operation x2 -> x0, local copies, waits for them, and re-layouts: 3.31 us -> none  [the longest x1 1.78 us: layer_grads(): block_output_gradient.reshape(sequence_count, SEQUENCE_TOKENS, KEY_VALUE_...]
    reduce_sum x1 -> x0, other arithmetic: 2.09 us -> none  [normalize(): jnp.mean(wide_inputs * wide_inputs, axis=-1, keepdims=True) + epsilon]
    reshape x2 -> x0, local copies, waits for them, and re-layouts: 1.77 us -> none  [the longest x1 1.71 us: layer_grads(): key_projected.reshape(sequence_count, SEQUENCE_TOKENS, KEY_VALUE_HEADS, H...]
where the time goes in v2:
time: 146 us; the launch traced here: 145 us
  Pallas kernels  136 us (93%)
  local copies, waits for them, and re-layouts  9.06 us (6%)
    pallas_call x1, Pallas kernels, per_device(): pl.pallas_call(lambda *refs: whole_kernel(replicas, sections, *refs), out...  136 us
    unnamed x7, local copies, waits for them, and re-layouts  9.06 us

profile of v2, /device:TPU:0, one launch (start us, length us, event | category | flops | bytes accessed | tf_op | source)
XLA Modules:
  0.0 145.4 jit_solution(11410068539152285761)
XLA Ops:
  0.6 135.7 %shard_map.94 = (bf16[1,4096,512]{2,1,0:T(8,128)(2,1)}, bf16[1,4096,512]{2,1,0:T(8,128)(2,1)}, bf16[1,256,4096]{2,1,0:T(8,128)(2,1)}) custom-call(bf16[1,256,4096]{2,1,0:T(8,128)(2,1)} %refs_0_.1, f32[1,4096]{1,0:T(1,128)} %refs_1_.1, bf16[1,256,2048]{2,1,0:T(8,128)(2,1)} %refs_2_.1, bf16[1,256,2048]{2,1,0:T(8,128)(2,1)} %refs_3_.1, ...), custom_call_target="tpu_custom_call" | custom-call | tf_op jit(solution)/shard_map/pallas_call | solution.py:360
  136.3 0.0 copy-start
  136.3 4.6 %copy.13 = bf16[1,4096,512]{2,1,0:T(8,128)(2,1)} copy(bf16[1,4096,512]{2,1,0:T(8,128)(2,1)} %get-tuple-element.6) | data formatting | bytes 8388608
  140.9 0.0 copy-done
  140.9 0.0 copy-start.1
  141.0 2.1 %copy.14 = bf16[1,4096,512]{2,1,0:T(8,128)(2,1)} copy(bf16[1,4096,512]{2,1,0:T(8,128)(2,1)S(1)} %copy-done) | data formatting | bytes 8388608
  143.1 1.0 copy-done.1
  144.1 1.3 copy.15
Async XLA Ops:
  136.3 4.6 %copy-start = (bf16[1,4096,512]{2,1,0:T(8,128)(2,1)S(1)}, bf16[1,4096,512]{2,1,0:T(8,128)(2,1)}, u32[]{:S(2)}) copy-start(bf16[1,4096,512]{2,1,0:T(8,128)(2,1)} %get-tuple-element.7) | copy-start | bytes 12582916
  140.9 3.1 %copy-start.1 = (bf16[1,256,4096]{2,1,0:T(8,128)(2,1)S(1)}, bf16[1,256,4096]{2,1,0:T(8,128)(2,1)}, u32[]{:S(2)}) copy-start(bf16[1,256,4096]{2,1,0:T(8,128)(2,1)} %get-tuple-element.8) | copy-start | bytes 6291460

commit v3 on v2

--- a/solution.py
+++ b/solution.py
@@ -13,15 +13,7 @@
 epsilon = 1e-05
 
 
-CHUNKS_PER_ARRAY = 4
-
-
-def bit_orders(bit_count, chunk_count):
-    plain = list(range(bit_count))
-    swapped = list(plain)
-    if bit_count >= 3:
-        swapped[1], swapped[2] = swapped[2], swapped[1]
-    return [swapped if chunk % 4 == 3 else plain for chunk in range(chunk_count)]
+MOST_CHUNKS = 8
 
 
 MESH = pl.DeviceIdType.MESH
@@ -29,8 +21,13 @@
 TERM_BLOCK = 256
 ROW_TILE = 16
 LOAD_PIECES = 4
-INPUT_TERM_STEP = 3
-FINAL_SUM_STEP = 10
+KEY_PASS_STEP = 3
+INPUT_TERM_STEP = 6
+FINAL_SUM_STEP = 20
+
+
+def chunks_of(rows, replicas):
+    return min(MOST_CHUNKS, rows // (ROW_TILE * replicas))
 
 
 def contract(left, right, left_axis, right_axis):
@@ -64,6 +61,7 @@
     grads,
     scaled,
     row_dot,
+    probabilities,
     outgoing,
     received,
     final,
@@ -75,14 +73,15 @@
     landing = rest[:bit_count]
     send_sem, recv_sem, store_sem, cot_sem, x_sem, weight_sem, load_sem = rest[bit_count:]
     rows = key_out.shape[1]
+    chunks_per_array = chunks_of(rows, replicas)
     tokens = x_held.shape[0]
     width = x_held.shape[1]
     group = query.shape[1] // KEY_VALUE_HEADS
     scale = HEAD_SIZE ** (-0.5)
-    chunk_rows = rows // CHUNKS_PER_ARRAY
-    chunk_count = 2 * CHUNKS_PER_ARRAY
+    chunk_rows = rows // chunks_per_array
+    chunk_count = 2 * chunks_per_array
     stage_count = 2 * bit_count
-    orders = bit_orders(bit_count, chunk_count)
+    orders = [list(range(bit_count))] * chunk_count
     section = lax.axis_index("section")
     me = lax.axis_index("dp")
     below = lax.rem(section + sections - 1, sections)
@@ -115,10 +114,11 @@
     for index in range(LOAD_PIECES):
         x_copy(index).start()
     for block in range(feature_blocks):
-        for which in range(2):
-            weight_copy(which, block).start()
+        weight_copy(0, block).start()
     query_copy.start()
     gradient_copy.start()
+    for block in range(feature_blocks):
+        weight_copy(1, block).start()
 
     barrier = pltpu.get_barrier_semaphore()
     for partner in partners:
@@ -141,22 +141,18 @@
             inv_rms[here] = inverse
             normed[here] = (wide * inverse * gain[...]).astype(jnp.bfloat16)
 
-    projected_wide[...] = jnp.zeros_like(projected_wide)
-
-    @pl.loop(0, feature_blocks)
-    def _(block):
-        here = pl.ds(pl.multiple_of(block * FEATURE_BLOCK, FEATURE_BLOCK), FEATURE_BLOCK)
-        for which in range(2):
+    def project(which):
+        projected_wide[...] = jnp.zeros_like(projected_wide)
+
+        @pl.loop(0, feature_blocks)
+        def _(block):
+            here = pl.ds(pl.multiple_of(block * FEATURE_BLOCK, FEATURE_BLOCK), FEATURE_BLOCK)
             weight_copy(which, block).wait()
-            projected_wide[which] += contract(normed[:, here], weights[which, here], 1, 0)
-
-    projected[...] = projected_wide[...].astype(jnp.bfloat16)
-    query_copy.wait()
-    gradient_copy.wait()
-    top_copy.start()
-
-    @pl.loop(0, tokens // SEQUENCE_TOKENS * KEY_VALUE_HEADS)
-    def _(index):
+            projected_wide[...] += contract(normed[:, here], weights[which, here], 1, 0)
+
+        projected[which] = projected_wide[...].astype(jnp.bfloat16)
+
+    def places(index):
         sequence = index // KEY_VALUE_HEADS
         head = lax.rem(index, KEY_VALUE_HEADS)
         here = pl.ds(pl.multiple_of(sequence * SEQUENCE_TOKENS, SEQUENCE_TOKENS), SEQUENCE_TOKENS)
@@ -171,21 +167,40 @@
                 axis=0,
             )
 
-        head_queries = stacked(query)
-        head_gradients = stacked(gradient)
-        scores = contract(head_queries, projected[0, here, column], 1, 1) * scale
-        query_row = lax.rem(lax.broadcasted_iota(jnp.int32, scores.shape, 0), SEQUENCE_TOKENS)
-        key_row = lax.broadcasted_iota(jnp.int32, scores.shape, 1)
-        scores = jnp.where(query_row >= key_row, scores, -1e30)
-        weight = jnp.exp(scores - jnp.max(scores, axis=-1, keepdims=True))
-        probability = weight * (1.0 / jnp.sum(weight, axis=-1, keepdims=True))
-        grads[1, here, column] = contract(
-            probability.astype(jnp.bfloat16), head_gradients, 0, 0
-        ).astype(jnp.bfloat16)
-        grad_prob = contract(head_gradients, projected[1, here, column], 1, 1)
-        row_delta = jnp.sum(probability * grad_prob, axis=-1, keepdims=True)
-        dscore = (probability * (grad_prob - row_delta) * scale).astype(jnp.bfloat16)
-        grads[0, here, column] = contract(dscore, head_queries, 0, 0).astype(jnp.bfloat16)
+        return here, column, stacked
+
+    head_count = tokens // SEQUENCE_TOKENS * KEY_VALUE_HEADS
+
+    def value_pass():
+        @pl.loop(0, head_count)
+        def _(index):
+            here, column, stacked = places(index)
+            scores = contract(stacked(query), projected[0, here, column], 1, 1) * scale
+            query_row = lax.rem(lax.broadcasted_iota(jnp.int32, scores.shape, 0), SEQUENCE_TOKENS)
+            key_row = lax.broadcasted_iota(jnp.int32, scores.shape, 1)
+            scores = jnp.where(query_row >= key_row, scores, -1e30)
+            weight = jnp.exp(scores - jnp.max(scores, axis=-1, keepdims=True))
+            probability = weight * (1.0 / jnp.sum(weight, axis=-1, keepdims=True))
+            probabilities[index] = probability
+            grads[1, here, column] = contract(
+                probability.astype(jnp.bfloat16), stacked(gradient), 0, 0
+            ).astype(jnp.bfloat16)
+
+    def key_pass():
+        @pl.loop(0, head_count)
+        def _(index):
+            here, column, stacked = places(index)
+            probability = probabilities[index]
+            grad_prob = contract(stacked(gradient), projected[1, here, column], 1, 1)
+            row_delta = jnp.sum(probability * grad_prob, axis=-1, keepdims=True)
+            dscore = (probability * (grad_prob - row_delta) * scale).astype(jnp.bfloat16)
+            grads[0, here, column] = contract(dscore, stacked(query), 0, 0).astype(jnp.bfloat16)
+
+    project(0)
+    query_copy.wait()
+    gradient_copy.wait()
+    value_pass()
+    top_copy.start()
 
     pl.semaphore_wait(barrier, bit_count + 2)
 
@@ -199,10 +214,10 @@
     )
 
     def target(chunk):
-        return (value_out, key_out)[chunk // CHUNKS_PER_ARRAY]
+        return (value_out, key_out)[chunk // chunks_per_array]
 
     def base(chunk):
-        return (chunk % CHUNKS_PER_ARRAY) * chunk_rows
+        return (chunk % chunks_per_array) * chunk_rows
 
     offsets = []
     for chunk in range(chunk_count):
@@ -214,7 +229,7 @@
         offsets.append(kept)
 
     def area(chunk, offset, size, buffer=held):
-        return buffer.at[chunk // CHUNKS_PER_ARRAY, pl.ds(pl.multiple_of(offset, 16), size)]
+        return buffer.at[chunk // chunks_per_array, pl.ds(pl.multiple_of(offset, 16), size)]
 
     def stage_copy(chunk, stage):
         if stage < bit_count:
@@ -248,7 +263,7 @@
     def add(chunk, stage):
         size = chunk_rows >> (stage + 1)
         tile = min(size, 32)
-        index = chunk // CHUNKS_PER_ARRAY
+        index = chunk // chunks_per_array
         start = offsets[chunk][stage + 1]
         is_final = stage == bit_count - 1
         result = gathered if is_final else held
@@ -274,8 +289,8 @@
             store_copy(chunk).start()
 
     def weight_term(chunk):
-        which = 1 - chunk // CHUNKS_PER_ARRAY
-        index = chunk // CHUNKS_PER_ARRAY
+        which = 1 - chunk // chunks_per_array
+        index = chunk // chunks_per_array
 
         @pl.loop(0, chunk_rows // TERM_BLOCK)
         def _(step):
@@ -328,7 +343,7 @@
 
         final_copy.start()
 
-    lags = [stage + (2 if stage else 1) for stage in range(stage_count)]
+    lags = [2 + 2 * stage if stage else 1 for stage in range(stage_count)]
     for step in range(chunk_count + lags[-1]):
         for stage in reversed(range(stage_count)):
             chunk = step - lags[stage]
@@ -337,6 +352,9 @@
         if step < chunk_count:
             weight_term(step)
             stage_copy(step, 0).start()
+        if step == KEY_PASS_STEP:
+            project(1)
+            key_pass()
         if step == INPUT_TERM_STEP:
             input_term()
         if step == FINAL_SUM_STEP:
@@ -352,7 +370,7 @@
     tokens, width = layer_inputs.shape[1:]
     rows, columns = w_key.shape[1:]
     bit_count = replicas.bit_length() - 1
-    chunk_count = 2 * CHUNKS_PER_ARRAY
+    chunk_count = 2 * chunks_of(rows, replicas)
     low = jnp.bfloat16
     wide = jnp.float32
     anywhere = pl.BlockSpec(memory_space=pl.ANY)
@@ -374,11 +392,19 @@
             pltpu.VMEM(queries.shape[1:], low),
             pltpu.VMEM((2, rows, columns), low),
             pltpu.VMEM((tokens, width), low),
-            pltpu.VMEM((2, tokens, columns), wide),
+            pltpu.VMEM((tokens, columns), wide),
             pltpu.VMEM((2, tokens, columns), low),
             pltpu.VMEM((2, tokens, columns), low),
             pltpu.VMEM((tokens, width), wide),
             pltpu.VMEM((tokens, 1), wide),
+            pltpu.VMEM(
+                (
+                    tokens // SEQUENCE_TOKENS * KEY_VALUE_HEADS,
+                    queries.shape[2] // columns * SEQUENCE_TOKENS,
+                    SEQUENCE_TOKENS,
+                ),
+                wide,
+            ),
             pltpu.VMEM((tokens, width), low),
             pltpu.VMEM((tokens, width), low),
             pltpu.VMEM((tokens, width), low),

time: 146 us -> 129 us (0.88)
  Pallas kernels: 136 us -> 120 us
    pallas_call x1, Pallas kernels: 136 us -> 120 us  [per_device(): pl.pallas_call(lambda *refs: whole_kernel(replicas, sections, *refs), out...]
where the time goes in v3:
time: 129 us
  Pallas kernels  120 us (93%)
  local copies, waits for them, and re-layouts  9.06 us (7%)
    pallas_call x1, Pallas kernels, per_device(): pl.pallas_call(lambda *refs: whole_kernel(replicas, sections, *refs), out...  120 us
    unnamed x7, local copies, waits for them, and re-layouts  9.06 us

profile of v3, /device:TPU:0, one launch (start us, length us, event | category | flops | bytes accessed | tf_op | source)
XLA Modules:
  0.0 129.2 jit_solution(1934124766948406761)
XLA Ops:
  0.6 119.5 %shard_map.94 = (bf16[1,4096,512]{2,1,0:T(8,128)(2,1)}, bf16[1,4096,512]{2,1,0:T(8,128)(2,1)}, bf16[1,256,4096]{2,1,0:T(8,128)(2,1)}) custom-call(bf16[1,256,4096]{2,1,0:T(8,128)(2,1)} %refs_0_.1, f32[1,4096]{1,0:T(1,128)} %refs_1_.1, bf16[1,256,2048]{2,1,0:T(8,128)(2,1)} %refs_2_.1, bf16[1,256,2048]{2,1,0:T(8,128)(2,1)} %refs_3_.1, ...), custom_call_target="tpu_custom_call" | custom-call | tf_op jit(solution)/shard_map/pallas_call | solution.py:378
  120.2 0.0 copy-start
  120.2 4.6 %copy.13 = bf16[1,4096,512]{2,1,0:T(8,128)(2,1)} copy(bf16[1,4096,512]{2,1,0:T(8,128)(2,1)} %get-tuple-element.6) | data formatting | bytes 8388608
  124.8 0.0 copy-done
  124.8 0.0 copy-start.1
  124.8 2.1 %copy.14 = bf16[1,4096,512]{2,1,0:T(8,128)(2,1)} copy(bf16[1,4096,512]{2,1,0:T(8,128)(2,1)S(1)} %copy-done) | data formatting | bytes 8388608
  127.0 1.0 copy-done.1
  127.9 1.3 %copy.15 = bf16[1,256,4096]{2,1,0:T(8,128)(2,1)} copy(bf16[1,256,4096]{2,1,0:T(8,128)(2,1)S(1)} %copy-done.1) | data formatting | bytes 4194304
Async XLA Ops:
  120.2 4.6 %copy-start = (bf16[1,4096,512]{2,1,0:T(8,128)(2,1)S(1)}, bf16[1,4096,512]{2,1,0:T(8,128)(2,1)}, u32[]{:S(2)}) copy-start(bf16[1,4096,512]{2,1,0:T(8,128)(2,1)} %get-tuple-element.7) | copy-start | bytes 12582916
  124.8 3.1 %copy-start.1 = (bf16[1,256,4096]{2,1,0:T(8,128)(2,1)S(1)}, bf16[1,256,4096]{2,1,0:T(8,128)(2,1)}, u32[]{:S(2)}) copy-start(bf16[1,256,4096]{2,1,0:T(8,128)(2,1)} %get-tuple-element.8) | copy-start | bytes 6291460
